TPU v7x, 32 devices: a whole 2x2x4 slice. The times are simulated.
32 devices in a mesh: ep: 4 (over y, x), fsdp: 8 (over z, core).
Axes of the slice: x: 2, y: 2, z: 4, core: 2. Of those that a mesh axis runs over, the one named last changes fastest.
Arguments:
- w_gate: float32 [64, 2048, 1024], P('ep', 'fsdp'), may hold values from -0.1875 to 0.1875
- avg_gate: bfloat16 [64, 2048, 1024], P('ep', 'fsdp'), may hold values from -0.0625 to 0.0625
- w_up: float32 [64, 2048, 1024], P('ep', 'fsdp'), may hold values from -0.1875 to 0.1875
- avg_up: bfloat16 [64, 2048, 1024], P('ep', 'fsdp'), may hold values from -0.0625 to 0.0625
- w_down: float32 [64, 1024, 2048], P('ep', None, 'fsdp'), may hold values from -0.25 to 0.25
- avg_down: bfloat16 [64, 1024, 2048], P('ep', None, 'fsdp'), may hold values from -0.09375 to 0.09375
- router_weight: float32 [2048, 64], P('fsdp', 'ep'), may hold values from -0.125 to 0.125
- router_gain: float32 [2048], P('fsdp'), may hold values from 0.25 to 1.75
Outputs:
- serve_gate: bfloat16 [64, 2048, 1024], P('ep', None, 'fsdp')
- serve_up: bfloat16 [64, 2048, 1024], P('ep', None, 'fsdp')
- serve_down: bfloat16 [64, 1024, 2048], P('ep', 'fsdp')
- scale_gate: float32 [64, 1024], P('ep', 'fsdp')
- scale_up: float32 [64, 1024], P('ep', 'fsdp')
- scale_down: float32 [64, 1024], P('ep', 'fsdp')
- serve_router: bfloat16 [2048, 64], replicated
All inputs are finite; a program needn't handle non-finite values.
Results may differ from a plain program's by a relative error of at most 0.001.
Values may be sent and summed in bfloat16 or wider, within the bound.
A program may use at most 192 MiB of HBM per device.

v0:
```python
import jax
import jax.numpy as jnp
from jax import lax
from jax.sharding import PartitionSpec as P


def on_device(w_gate, avg_gate, w_up, avg_up, w_down, avg_down, router_weight, router_gain):
    fresh_gate = w_gate + avg_gate.astype(jnp.float32)
    fresh_up = w_up + avg_up.astype(jnp.float32)
    fresh_down = w_down + avg_down.astype(jnp.float32)
    total_gate, total_up, total_down = lax.psum(
        (
            jnp.sum(fresh_gate * fresh_gate, axis=1),
            jnp.sum(fresh_up * fresh_up, axis=1),
            jnp.sum(fresh_down * fresh_down, axis=2),
        ),
        "fsdp",
    )
    scale_gate = jnp.sqrt(total_gate)
    scale_up = jnp.sqrt(total_up)
    scale_down = jnp.sqrt(total_down)
    narrow_gate, narrow_up, narrow_down = (
        (fresh_gate / jnp.expand_dims(scale_gate, 1)).astype(jnp.bfloat16),
        (fresh_up / jnp.expand_dims(scale_up, 1)).astype(jnp.bfloat16),
        (fresh_down / jnp.expand_dims(scale_down, 2)).astype(jnp.bfloat16),
    )
    serve_gate, serve_up = (
        lax.all_to_all(narrow_gate, "fsdp", split_axis=2, concat_axis=1, tiled=True),
        lax.all_to_all(narrow_up, "fsdp", split_axis=2, concat_axis=1, tiled=True),
    )
    serve_down = lax.all_to_all(narrow_down, "fsdp", split_axis=1, concat_axis=2, tiled=True)
    scale_gate = lax.dynamic_slice_in_dim(
        scale_gate, lax.axis_index("fsdp") * serve_gate.shape[2], serve_gate.shape[2], axis=1
    )
    scale_up = lax.dynamic_slice_in_dim(
        scale_up, lax.axis_index("fsdp") * serve_up.shape[2], serve_up.shape[2], axis=1
    )
    scale_down = lax.dynamic_slice_in_dim(
        scale_down, lax.axis_index("fsdp") * serve_down.shape[1], serve_down.shape[1], axis=1
    )
    part_router = (router_weight * router_gain[:, None]).astype(jnp.bfloat16)
    row_router = lax.all_gather(part_router, "fsdp", axis=0, tiled=True)
    serve_router = lax.all_gather(row_router, "ep", axis=1, tiled=True)
    return (serve_gate, serve_up, serve_down, scale_gate, scale_up, scale_down, serve_router)


def solution(mesh):
    placed = (
        P("ep", "fsdp", None),
        P("ep", "fsdp", None),
        P("ep", "fsdp", None),
        P("ep", "fsdp", None),
        P("ep", None, "fsdp"),
        P("ep", None, "fsdp"),
        P("fsdp", "ep"),
        P("fsdp"),
    )
    return jax.shard_map(
        on_device,
        mesh=mesh,
        in_specs=placed,
        out_specs=(
            P("ep", None, "fsdp"),
            P("ep", None, "fsdp"),
            P("ep", "fsdp", None),
            P("ep", "fsdp"),
            P("ep", "fsdp"),
            P("ep", "fsdp"),
            P(),
        ),
        check_vma=False,
    )
```

profile of v0, /device:TPU:0, one launch (start us, length us, event | category | flops | bytes accessed | tf_op | source)
XLA Modules:
  0.0 824.8 jit_solution(4685212397091970850)
XLA Ops:
  7.2 0.0 all-reduce.3.cloned.1.call-start
  7.2 17.6 %copy.31 = f32[16,256,1024]{1,0,2:T(8,128)} copy(f32[16,256,1024]{2,1,0:T(8,128)} %param.8) | data formatting | bytes 33554432 | tf_op args[0]
  24.8 17.6 %copy.34 = f32[16,256,1024]{1,0,2:T(8,128)} copy(f32[16,256,1024]{2,1,0:T(8,128)} %param.10) | data formatting | bytes 33554432 | tf_op args[2]
  42.4 12.5 %copy.30 = bf16[16,256,1024]{1,0,2:T(8,128)(2,1)} copy(bf16[16,256,1024]{2,1,0:T(8,128)(2,1)} %param.9) | data formatting | bytes 16777216 | tf_op args[1]
  54.9 12.5 %copy.33 = bf16[16,256,1024]{1,0,2:T(8,128)(2,1)} copy(bf16[16,256,1024]{2,1,0:T(8,128)(2,1)} %param.11) | data formatting | bytes 16777216 | tf_op args[3]
  67.4 0.0 copy-start
  67.4 0.0 copy-start.1
  67.4 25.2 %multiply_reduce_fusion = f32[16,1024]{0,1:T(8,128)} fusion(f32[16,1024,256]{2,1,0:T(8,128)} %param.12, bf16[16,1024,256]{2,1,0:T(8,128)(2,1)} %param.13), kind=kLoop, calls=%fused_computation.2 | loop fusion | flops 16760832 | bytes 25231360 | tf_op jit(solution)/shard_map/reduce_sum | solution.py:15
  92.6 0.0 copy-done
  92.6 0.0 copy-done.1
  92.6 13.2 %multiply_reduce_fusion.1 = (f32[16,1024]{0,1:T(8,128)}, f32[16,1024]{0,1:T(8,128)}) fusion(f32[16,256,1024]{1,0,2:T(8,128)} %copy.34, bf16[16,256,1024]{1,0,2:T(8,128)(2,1)S(1)} %copy-done.1, f32[16,256,1024]{1,0,2:T(8,128)} %copy.31, bf16[16,256,1024]{1,0,2:T(8,128)(2,1)S(1)} %copy-done), kind=kLoop, calls=%fused_computation.4 | loop fusion | flops 33521664 | bytes 50462720 | tf_op jit(solution)/shard_map/reduce_sum | solution.py:14
  105.8 0.0 all-reduce.3.cloned.1.call-update
  105.8 65.1 %all-reduce.3.cloned.1.call-done = (f32[16,1024]{0,1:T(8,128)}, f32[16,1024]{0,1:T(8,128)}, f32[16,1024]{0,1:T(8,128)}) async-done(((f32[16,1024]{0,1:T(8,128)}, f32[16,1024]{0,1:T(8,128)}, f32[16,1024]{0,1:T(8,128)}), (f32[16,1024]{0,1:T(8,128)}, f32[16,1024]{0,1:T(8,128)}, f32[16,1024]{0,1:T(8,128)})) %all-reduce.3.cloned.1.call-update) | async-done | bytes 196624 | tf_op jit(solution)/shard_map/psum | solution.py:11
  170.9 1.2 sqrt.10
  172.1 12.0 %divide_convert_fusion.1 = bf16[16,256,1024]{1,0,2:T(8,128)(2,1)} fusion(f32[16,256,1024]{1,0,2:T(8,128)} %copy.34, bf16[16,256,1024]{1,0,2:T(8,128)(2,1)} %copy.33, f32[16,1024]{0,1:T(8,128)S(1)} %sqrt.10), kind=kLoop, calls=%fused_computation.3 | loop fusion | flops 16777216 | bytes 33619968 | tf_op jit(solution)/shard_map/convert_element_type | solution.py:24
  184.1 0.0 copy-start.3
  184.1 5.1 all-to-all-start.1
  189.2 0.0 copy-done.3
  189.2 0.1 sqrt.9
  189.3 12.0 %divide_convert_fusion.2 = bf16[16,256,1024]{1,0,2:T(8,128)(2,1)} fusion(f32[16,256,1024]{1,0,2:T(8,128)} %copy.31, bf16[16,256,1024]{1,0,2:T(8,128)(2,1)} %copy.30, f32[16,1024]{0,1:T(8,128)S(1)} %sqrt.9), kind=kLoop, calls=%fused_computation.6 | loop fusion | flops 16777216 | bytes 33619968 | tf_op jit(solution)/shard_map/convert_element_type | solution.py:23
  201.3 0.0 copy-start.2
  201.3 171.7 %all-to-all-done.1 = bf16[16,256,1024]{1,0,2:T(8,128)(2,1)} async-done(((bf16[16,256,1024]{1,0,2:T(8,128)(2,1)}), bf16[16,256,1024]{1,0,2:T(8,128)(2,1)}, u32[]{:S(2)}, u32[]{:S(2)}) %all-to-all-start.1) | async-done | bytes 8388640 | tf_op jit(solution)/shard_map/all_to_all | solution.py:29
  373.0 5.1 all-to-all-start
  378.2 0.0 copy-done.2
  378.2 0.1 sqrt.11
  378.3 23.8 %divide_convert_fusion = bf16[16,1024,256]{2,0,1:T(8,128)(2,1)} fusion(f32[16,1024,256]{2,1,0:T(8,128)} %param.12, f32[16,1024]{0,1:T(8,128)S(1)} %sqrt.11, bf16[16,1024,256]{2,1,0:T(8,128)(2,1)} %param.13), kind=kLoop, calls=%fused_computation.1 | loop fusion | flops 16777216 | bytes 33619968 | tf_op jit(solution)/shard_map/convert_element_type | solution.py:25
  402.1 0.0 copy-start.4
  402.1 0.0 copy-start.5
  402.1 159.8 %all-to-all-done = bf16[16,256,1024]{1,0,2:T(8,128)(2,1)} async-done(((bf16[16,256,1024]{1,0,2:T(8,128)(2,1)}), bf16[16,256,1024]{1,0,2:T(8,128)(2,1)}, u32[]{:S(2)}, u32[]{:S(2)}) %all-to-all-start) | async-done | bytes 8388640 | tf_op jit(solution)/shard_map/all_to_all | solution.py:28
  561.8 5.0 all-to-all-start.2
  566.9 0.0 copy-done.4
  566.9 0.0 copy-done.5
  566.9 189.9 %all_gather.6 = bf16[2048,16]{0,1:T(8,128)(2,1)S(1)} all-gather(bf16[256,16]{0,1:T(8,128)(2,1)S(1)} %multiply_convert_fusion), channel_id=1, replica_groups=mesh['ep'=4,'fsdp'=8] {'fsdp'}, dimensions={0}, use_global_device_ids=true | all-gather | bytes 73728 | tf_op jit(solution)/shard_map/all_gather | solution.py:42
  756.8 9.1 %all_gather.7 = bf16[2048,64]{0,1:T(8,128)(2,1)S(1)} all-gather(bf16[2048,16]{0,1:T(8,128)(2,1)S(1)} %all_gather.6), channel_id=1, replica_groups=mesh['ep'=4,'fsdp'=8] {'ep'}, dimensions={1}, use_global_device_ids=true | all-gather | bytes 327680 | tf_op jit(solution)/shard_map/all_gather | solution.py:43
  765.9 0.7 copy.39
  766.6 0.7 copy.40
  767.3 0.7 copy.41
  767.9 12.3 %copy.35 = bf16[16,8,256,128]{3,2,1,0:T(8,128)(2,1)} copy(bf16[16,8,256,128]{2,0,3,1:T(8,128)(2,1)} %bitcast.4) | data formatting | bytes 16777216 | tf_op jit(solution)/shard_map/all_to_all | solution.py:29
  780.2 12.3 %copy.32 = bf16[16,8,256,128]{3,2,1,0:T(8,128)(2,1)} copy(bf16[16,8,256,128]{2,0,3,1:T(8,128)(2,1)} %bitcast.1) | data formatting | bytes 16777216 | tf_op jit(solution)/shard_map/all_to_all | solution.py:28
  792.5 0.0 all-to-all-done.2
  792.5 11.4 %copy.38 = bf16[16,128,8,256]{3,2,1,0:T(8,128)(2,1)} copy(bf16[16,128,8,256]{3,0,1,2:T(8,128)(2,1)} %bitcast.7) | data formatting | bytes 16777216 | tf_op jit(solution)/shard_map/all_to_all | solution.py:31
  803.9 13.4 %all_to_all.50 = bf16[16,128,2048]{2,1,0:T(8,128)(2,1)} reshape(bf16[16,128,8,256]{3,2,1,0:T(8,128)(2,1)} %copy.38) | data formatting | bytes 16777216 | tf_op jit(solution)/shard_map/all_to_all | solution.py:31
  817.3 0.7 copy.53
  (4 shorter events, 0.0 us)
Async XLA Ops:
  7.2 163.7 %all-reduce.3.cloned.1.call-start = ((), (), s32[]{:S(2)}) async-start(), calls=%async_computation.3 | async-start | bytes 3145728 | tf_op jit(solution)/shard_map/psum | solution.py:11
  67.4 25.2 %copy-start = (bf16[16,256,1024]{1,0,2:T(8,128)(2,1)S(1)}, bf16[16,256,1024]{1,0,2:T(8,128)(2,1)}, u32[]{:S(2)}) copy-start(bf16[16,256,1024]{1,0,2:T(8,128)(2,1)} %copy.30) | copy-start | bytes 25165828
  67.4 25.2 %copy-start.1 = (bf16[16,256,1024]{1,0,2:T(8,128)(2,1)S(1)}, bf16[16,256,1024]{1,0,2:T(8,128)(2,1)}, u32[]{:S(2)}) copy-start(bf16[16,256,1024]{1,0,2:T(8,128)(2,1)} %copy.33) | copy-start | bytes 25165828
  184.1 5.1 copy-start.3
  184.1 189.0 %all-to-all-start.1 = ((bf16[16,256,1024]{1,0,2:T(8,128)(2,1)}), bf16[16,256,1024]{1,0,2:T(8,128)(2,1)}, u32[]{:S(2)}, u32[]{:S(2)}) async-start(bf16[16,256,1024]{1,0,2:T(8,128)(2,1)} %divide_convert_fusion.1), calls=%async_computation.1 | async-start | bytes 16777216 | tf_op jit(solution)/shard_map/all_to_all | solution.py:29
  201.3 176.9 %copy-start.2 = (f32[16,1024]{0,1:T(8,128)S(1)}, f32[16,1024]{0,1:T(8,128)}, u32[]{:S(2)}) copy-start(f32[16,1024]{0,1:T(8,128)} %get-tuple-element.16) | copy-start | bytes 196612
  373.0 188.8 %all-to-all-start = ((bf16[16,256,1024]{1,0,2:T(8,128)(2,1)}), bf16[16,256,1024]{1,0,2:T(8,128)(2,1)}, u32[]{:S(2)}, u32[]{:S(2)}) async-start(bf16[16,256,1024]{1,0,2:T(8,128)(2,1)} %divide_convert_fusion.2), calls=%async_computation | async-start | bytes 16777216 | tf_op jit(solution)/shard_map/all_to_all | solution.py:28
  402.1 164.8 %copy-start.4 = (f32[256,16]{0,1:T(8,128)S(1)}, f32[256,16]{0,1:T(8,128)}, u32[]{:S(2)}) copy-start(f32[256,16]{0,1:T(8,128)} %param.14) | copy-start | bytes 49156
  402.1 164.8 %copy-start.5 = (f32[256]{0:T(256)S(1)}, f32[256]{0:T(256)}, u32[]{:S(2)}) copy-start(f32[256]{0:T(256)} %param.15) | copy-start | bytes 3076
  561.8 230.7 %all-to-all-start.2 = ((bf16[16,1024,256]{2,0,1:T(8,128)(2,1)}), bf16[16,1024,256]{2,0,1:T(8,128)(2,1)}, u32[]{:S(2)}, u32[]{:S(2)}) async-start(bf16[16,1024,256]{2,0,1:T(8,128)(2,1)} %divide_convert_fusion), calls=%async_computation.2 | async-start | bytes 16777216 | tf_op jit(solution)/shard_map/all_to_all | solution.py:31
Sparse Core Ops, SparseCore 0:
  105.9 64.9 all-reduce.2
where the time goes:
time: 827 us; the launch traced here: 825 us
  waiting for transfers between devices  397 us (48%)
  blocking collectives  199 us (24%)
  local copies, waits for them, and re-layouts  114 us (14%)
  other arithmetic  86.1 us (10%)
  starting transfers between devices  15.3 us (2%)
  between operations  14.1 us (2%)
    all_gather x1, blocking collectives, on_device(): row_router = lax.all_gather(part_router, 'fsdp', axis=0, tiled=True)  190 us
    all_to_all x1, waiting for transfers between devices, on_device(): lax.all_to_all(narrow_up, 'fsdp', split_axis=2, concat_axis=1, tiled=True)  172 us
    all_to_all x1, waiting for transfers between devices, on_device(): lax.all_to_all(narrow_gate, 'fsdp', split_axis=2, concat_axis=1, tiled=True)  160 us
    psum x1, waiting for transfers between devices, on_device(): lax.psum((jnp.sum(fresh_gate * fresh_gate, axis=1), jnp.sum(fresh_up * fr...  65.1 us
    unnamed x20, local copies, waits for them, and re-layouts  62.9 us
    reduce_sum x1, other arithmetic, on_device(): jnp.sum(fresh_down * fresh_down, axis=2)  25.2 us
    all_to_all x2, local copies, waits for them, and re-layouts, on_device(): lax.all_to_all(narrow_down, 'fsdp', split_axis=1, concat_axis=2, tiled=True)  24.8 us
    convert_element_type x1, other arithmetic, on_device(): (fresh_down / jnp.expand_dims(scale_down, 2)).astype(jnp.bfloat16)  23.8 us
  transfers between devices with their start and end apart: 4, of which 3 were waited for; matrix products, arithmetic and copies ran while one was open for 8% of the time, Pallas kernels for 0%

commit v1 on v0

--- a/solution.py
+++ b/solution.py
@@ -40,7 +40,7 @@
     )
     part_router = (router_weight * router_gain[:, None]).astype(jnp.bfloat16)
     row_router = lax.all_gather(part_router, "fsdp", axis=0, tiled=True)
-    serve_router = lax.all_gather(row_router, "ep", axis=1, tiled=True)
+    serve_router = jnp.concatenate(lax.all_gather(row_router, "ep"), axis=1)
     return (serve_gate, serve_up, serve_down, scale_gate, scale_up, scale_down, serve_router)
 
 

time: 827 us -> 827 us (level)
    unnamed x20 -> x19, local copies, waits for them, and re-layouts: 62.9 us -> 62.2 us
where the time goes in v1:
time: 827 us; the launch traced here: 825 us
  waiting for transfers between devices  397 us (48%)
  blocking collectives  199 us (24%)
  local copies, waits for them, and re-layouts  114 us (14%)
  other arithmetic  86.1 us (10%)
  starting transfers between devices  15.3 us (2%)
  between operations  14.1 us (2%)
    all_gather x1, blocking collectives, on_device(): row_router = lax.all_gather(part_router, 'fsdp', axis=0, tiled=True)  190 us
    all_to_all x1, waiting for transfers between devices, on_device(): lax.all_to_all(narrow_up, 'fsdp', split_axis=2, concat_axis=1, tiled=True)  172 us
    all_to_all x1, waiting for transfers between devices, on_device(): lax.all_to_all(narrow_gate, 'fsdp', split_axis=2, concat_axis=1, tiled=True)  160 us
    psum x1, waiting for transfers between devices, on_device(): lax.psum((jnp.sum(fresh_gate * fresh_gate, axis=1), jnp.sum(fresh_up * fr...  65.1 us
    unnamed x19, local copies, waits for them, and re-layouts  62.2 us
    reduce_sum x1, other arithmetic, on_device(): jnp.sum(fresh_down * fresh_down, axis=2)  25.2 us
    all_to_all x2, local copies, waits for them, and re-layouts, on_device(): lax.all_to_all(narrow_down, 'fsdp', split_axis=1, concat_axis=2, tiled=True)  24.8 us
    convert_element_type x1, other arithmetic, on_device(): (fresh_down / jnp.expand_dims(scale_down, 2)).astype(jnp.bfloat16)  23.8 us
  transfers between devices with their start and end apart: 4, of which 3 were waited for; matrix products, arithmetic and copies ran while one was open for 8% of the time, Pallas kernels for 0%

profile of v1, /device:TPU:0, one launch (start us, length us, event | category | flops | bytes accessed | tf_op | source)
XLA Modules:
  0.0 824.9 jit_solution(16867725516739927224)
XLA Ops:
  7.2 0.0 all-reduce.3.cloned.1.call-start
  7.2 17.6 %copy.33 = f32[16,256,1024]{1,0,2:T(8,128)} copy(f32[16,256,1024]{2,1,0:T(8,128)} %param.8) | data formatting | bytes 33554432 | tf_op args[0]
  24.8 17.6 %copy.36 = f32[16,256,1024]{1,0,2:T(8,128)} copy(f32[16,256,1024]{2,1,0:T(8,128)} %param.10) | data formatting | bytes 33554432 | tf_op args[2]
  42.4 12.5 %copy.32 = bf16[16,256,1024]{1,0,2:T(8,128)(2,1)} copy(bf16[16,256,1024]{2,1,0:T(8,128)(2,1)} %param.9) | data formatting | bytes 16777216 | tf_op args[1]
  54.9 12.5 %copy.35 = bf16[16,256,1024]{1,0,2:T(8,128)(2,1)} copy(bf16[16,256,1024]{2,1,0:T(8,128)(2,1)} %param.11) | data formatting | bytes 16777216 | tf_op args[3]
  67.4 0.0 copy-start
  67.4 0.0 copy-start.1
  67.4 25.2 %multiply_reduce_fusion = f32[16,1024]{0,1:T(8,128)} fusion(f32[16,1024,256]{2,1,0:T(8,128)} %param.12, bf16[16,1024,256]{2,1,0:T(8,128)(2,1)} %param.13), kind=kLoop, calls=%fused_computation.2 | loop fusion | flops 16760832 | bytes 25231360 | tf_op jit(solution)/shard_map/reduce_sum | solution.py:15
  92.6 0.0 copy-done
  92.6 0.0 copy-done.1
  92.6 13.2 %multiply_reduce_fusion.1 = (f32[16,1024]{0,1:T(8,128)}, f32[16,1024]{0,1:T(8,128)}) fusion(f32[16,256,1024]{1,0,2:T(8,128)} %copy.36, bf16[16,256,1024]{1,0,2:T(8,128)(2,1)S(1)} %copy-done.1, f32[16,256,1024]{1,0,2:T(8,128)} %copy.33, bf16[16,256,1024]{1,0,2:T(8,128)(2,1)S(1)} %copy-done), kind=kLoop, calls=%fused_computation.4 | loop fusion | flops 33521664 | bytes 50462720 | tf_op jit(solution)/shard_map/reduce_sum | solution.py:14
  105.8 0.0 all-reduce.3.cloned.1.call-update
  105.8 65.1 %all-reduce.3.cloned.1.call-done = (f32[16,1024]{0,1:T(8,128)}, f32[16,1024]{0,1:T(8,128)}, f32[16,1024]{0,1:T(8,128)}) async-done(((f32[16,1024]{0,1:T(8,128)}, f32[16,1024]{0,1:T(8,128)}, f32[16,1024]{0,1:T(8,128)}), (f32[16,1024]{0,1:T(8,128)}, f32[16,1024]{0,1:T(8,128)}, f32[16,1024]{0,1:T(8,128)})) %all-reduce.3.cloned.1.call-update) | async-done | bytes 196624 | tf_op jit(solution)/shard_map/psum | solution.py:11
  170.9 1.2 sqrt.10
  172.1 12.0 %divide_convert_fusion.1 = bf16[16,256,1024]{1,0,2:T(8,128)(2,1)} fusion(f32[16,256,1024]{1,0,2:T(8,128)} %copy.36, bf16[16,256,1024]{1,0,2:T(8,128)(2,1)} %copy.35, f32[16,1024]{0,1:T(8,128)S(1)} %sqrt.10), kind=kLoop, calls=%fused_computation.3 | loop fusion | flops 16777216 | bytes 33619968 | tf_op jit(solution)/shard_map/convert_element_type | solution.py:24
  184.1 0.0 copy-start.3
  184.1 5.1 all-to-all-start.1
  189.2 0.0 copy-done.3
  189.2 0.1 sqrt.9
  189.3 12.0 %divide_convert_fusion.2 = bf16[16,256,1024]{1,0,2:T(8,128)(2,1)} fusion(f32[16,256,1024]{1,0,2:T(8,128)} %copy.33, bf16[16,256,1024]{1,0,2:T(8,128)(2,1)} %copy.32, f32[16,1024]{0,1:T(8,128)S(1)} %sqrt.9), kind=kLoop, calls=%fused_computation.6 | loop fusion | flops 16777216 | bytes 33619968 | tf_op jit(solution)/shard_map/convert_element_type | solution.py:23
  201.3 0.0 copy-start.2
  201.3 171.7 %all-to-all-done.1 = bf16[16,256,1024]{1,0,2:T(8,128)(2,1)} async-done(((bf16[16,256,1024]{1,0,2:T(8,128)(2,1)}), bf16[16,256,1024]{1,0,2:T(8,128)(2,1)}, u32[]{:S(2)}, u32[]{:S(2)}) %all-to-all-start.1) | async-done | bytes 8388640 | tf_op jit(solution)/shard_map/all_to_all | solution.py:29
  373.0 5.1 all-to-all-start
  378.2 0.0 copy-done.2
  378.2 0.1 sqrt.11
  378.3 23.8 %divide_convert_fusion = bf16[16,1024,256]{2,0,1:T(8,128)(2,1)} fusion(f32[16,1024,256]{2,1,0:T(8,128)} %param.12, f32[16,1024]{0,1:T(8,128)S(1)} %sqrt.11, bf16[16,1024,256]{2,1,0:T(8,128)(2,1)} %param.13), kind=kLoop, calls=%fused_computation.1 | loop fusion | flops 16777216 | bytes 33619968 | tf_op jit(solution)/shard_map/convert_element_type | solution.py:25
  402.1 0.0 copy-start.4
  402.1 0.0 copy-start.5
  402.1 159.8 %all-to-all-done = bf16[16,256,1024]{1,0,2:T(8,128)(2,1)} async-done(((bf16[16,256,1024]{1,0,2:T(8,128)(2,1)}), bf16[16,256,1024]{1,0,2:T(8,128)(2,1)}, u32[]{:S(2)}, u32[]{:S(2)}) %all-to-all-start) | async-done | bytes 8388640 | tf_op jit(solution)/shard_map/all_to_all | solution.py:28
  561.8 5.0 all-to-all-start.2
  566.9 0.0 copy-done.4
  566.9 0.0 copy-done.5
  566.9 189.9 %all_gather.9 = bf16[2048,16]{0,1:T(8,128)(2,1)S(1)} all-gather(bf16[256,16]{0,1:T(8,128)(2,1)S(1)} %multiply_convert_fusion), channel_id=1, replica_groups=mesh['ep'=4,'fsdp'=8] {'fsdp'}, dimensions={0}, use_global_device_ids=true | all-gather | bytes 73728 | tf_op jit(solution)/shard_map/all_gather | solution.py:42
  756.8 9.1 %all-gather = bf16[8192,16]{0,1:T(8,128)(2,1)S(1)} all-gather(bf16[2048,16]{0,1:T(8,128)(2,1)S(1)} %all_gather.9), channel_id=2, replica_groups=mesh['ep'=4,'fsdp'=8] {'ep'}, dimensions={0}, use_global_device_ids=true | all-gather | bytes 327680 | tf_op jit(solution)/shard_map/all_gather | solution.py:43
  765.9 0.7 copy.54
  766.6 0.7 copy.42
  767.3 0.7 copy.43
  768.0 0.7 copy.44
  768.6 12.3 %copy.37 = bf16[16,8,256,128]{3,2,1,0:T(8,128)(2,1)} copy(bf16[16,8,256,128]{2,0,3,1:T(8,128)(2,1)} %bitcast.4) | data formatting | bytes 16777216 | tf_op jit(solution)/shard_map/all_to_all | solution.py:29
  780.9 12.3 %copy.34 = bf16[16,8,256,128]{3,2,1,0:T(8,128)(2,1)} copy(bf16[16,8,256,128]{2,0,3,1:T(8,128)(2,1)} %bitcast.1) | data formatting | bytes 16777216 | tf_op jit(solution)/shard_map/all_to_all | solution.py:28
  793.2 0.0 all-to-all-done.2
  793.2 11.4 %copy.40 = bf16[16,128,8,256]{3,2,1,0:T(8,128)(2,1)} copy(bf16[16,128,8,256]{3,0,1,2:T(8,128)(2,1)} %bitcast.7) | data formatting | bytes 16777216 | tf_op jit(solution)/shard_map/all_to_all | solution.py:31
  804.6 13.4 %all_to_all.50 = bf16[16,128,2048]{2,1,0:T(8,128)(2,1)} reshape(bf16[16,128,8,256]{3,2,1,0:T(8,128)(2,1)} %copy.40) | data formatting | bytes 16777216 | tf_op jit(solution)/shard_map/all_to_all | solution.py:31
  (4 shorter events, 0.0 us)
Async XLA Ops:
  7.2 163.7 %all-reduce.3.cloned.1.call-start = ((), (), s32[]{:S(2)}) async-start(), calls=%async_computation.3 | async-start | bytes 3145728 | tf_op jit(solution)/shard_map/psum | solution.py:11
  67.4 25.2 %copy-start = (bf16[16,256,1024]{1,0,2:T(8,128)(2,1)S(1)}, bf16[16,256,1024]{1,0,2:T(8,128)(2,1)}, u32[]{:S(2)}) copy-start(bf16[16,256,1024]{1,0,2:T(8,128)(2,1)} %copy.32) | copy-start | bytes 25165828
  67.4 25.2 %copy-start.1 = (bf16[16,256,1024]{1,0,2:T(8,128)(2,1)S(1)}, bf16[16,256,1024]{1,0,2:T(8,128)(2,1)}, u32[]{:S(2)}) copy-start(bf16[16,256,1024]{1,0,2:T(8,128)(2,1)} %copy.35) | copy-start | bytes 25165828
  184.1 5.1 copy-start.3
  184.1 189.0 %all-to-all-start.1 = ((bf16[16,256,1024]{1,0,2:T(8,128)(2,1)}), bf16[16,256,1024]{1,0,2:T(8,128)(2,1)}, u32[]{:S(2)}, u32[]{:S(2)}) async-start(bf16[16,256,1024]{1,0,2:T(8,128)(2,1)} %divide_convert_fusion.1), calls=%async_computation.1 | async-start | bytes 16777216 | tf_op jit(solution)/shard_map/all_to_all | solution.py:29
  201.3 176.9 %copy-start.2 = (f32[16,1024]{0,1:T(8,128)S(1)}, f32[16,1024]{0,1:T(8,128)}, u32[]{:S(2)}) copy-start(f32[16,1024]{0,1:T(8,128)} %get-tuple-element.16) | copy-start | bytes 196612
  373.0 188.8 %all-to-all-start = ((bf16[16,256,1024]{1,0,2:T(8,128)(2,1)}), bf16[16,256,1024]{1,0,2:T(8,128)(2,1)}, u32[]{:S(2)}, u32[]{:S(2)}) async-start(bf16[16,256,1024]{1,0,2:T(8,128)(2,1)} %divide_convert_fusion.2), calls=%async_computation | async-start | bytes 16777216 | tf_op jit(solution)/shard_map/all_to_all | solution.py:28
  402.1 164.8 %copy-start.4 = (f32[256,16]{0,1:T(8,128)S(1)}, f32[256,16]{0,1:T(8,128)}, u32[]{:S(2)}) copy-start(f32[256,16]{0,1:T(8,128)} %param.14) | copy-start | bytes 49156
  402.1 164.8 %copy-start.5 = (f32[256]{0:T(256)S(1)}, f32[256]{0:T(256)}, u32[]{:S(2)}) copy-start(f32[256]{0:T(256)} %param.15) | copy-start | bytes 3076
  561.8 231.4 %all-to-all-start.2 = ((bf16[16,1024,256]{2,0,1:T(8,128)(2,1)}), bf16[16,1024,256]{2,0,1:T(8,128)(2,1)}, u32[]{:S(2)}, u32[]{:S(2)}) async-start(bf16[16,1024,256]{2,0,1:T(8,128)(2,1)} %divide_convert_fusion), calls=%async_computation.2 | async-start | bytes 16777216 | tf_op jit(solution)/shard_map/all_to_all | solution.py:31
Sparse Core Ops, SparseCore 0:
  105.9 64.9 all-reduce.2
